TPU v7x, 32 devices: a whole 2x2x4 slice. The times are simulated.
32 devices in a mesh: gx: 8 (over z, y), gy: 4 (over x, core).
Axes of the slice: x: 2, y: 2, z: 4, core: 2. Of those that a mesh axis runs over, the one named last changes fastest.
Arguments:
- anomalies: float32 [80, 16, 32, 128], P(None, 'gx', 'gy'), may hold values from -6 to 6
- state_mean: float32 [16, 32, 128], P('gx', 'gy'), may hold values from -6 to 6
- obs_value: float32 [16, 256], P(None, 'gy'), may hold values from -8 to 8
- obs_cell: int32 [16, 256], replicated, may hold values from 0 to 2047
- owner: int32 [16], replicated, may hold values from 0 to 7, as said below
- order: int32 [16], replicated, may hold values from 0 to 15, each once
- root_inv: float32 [16, 256, 256], P(None, 'gy'), as said below
- gain_inv: float32 [16, 256, 256], P(None, 'gy'), as said below
Outputs:
- post_anomalies: float32 [80, 16, 32, 128], P(None, 'gx', 'gy')
- post_mean: float32 [16, 32, 128], P('gx', 'gy')
Inputs may be any that keep to these rules, and one draw needn't show every extreme that they name: `owner`: some batch lies at slab 8 - 2, some at slab 1 and some at slab 8 // 2; the others favour low slabs. `order`: each batch number once. `root_inv`: symmetric. `gain_inv`: symmetric.
All inputs are finite; a program needn't handle non-finite values.
Results may differ from a plain program's by a relative error of at most 0.0001.
Values sent between devices are 32-bit elements; how exact they have to be, the bound alone decides.
A program may use at most 64 MiB of HBM per device.

v0:
```python
import jax
import jax.numpy as jnp
from jax import lax
from jax.sharding import PartitionSpec as P

BATCHES = 16
REACH = 3


def shifted(value, axis, steps):
    count = lax.axis_size(axis)
    pairs = [(source, (source + steps) % count) for source in range(count)]
    return lax.ppermute(value, axis, pairs)


def product(left_side, right_side):
    return jnp.dot(
        left_side, right_side, precision=lax.Precision.HIGHEST, preferred_element_type=jnp.float32
    )


def prior_direct(masked):
    total = masked
    for step in range(1, REACH + 1):
        for sign_step in [step, -step]:
            total = total + shifted(masked, "gx", sign_step)
    return total


def local(anomalies, state_mean, obs_value, obs_cell, owner, order, root_inv, gain_inv):
    members, lon_dev, lat_dev, levels = anomalies.shape
    cell_count = lon_dev * lat_dev * levels
    quarter = obs_value.shape[1]
    obs_total = obs_cell.shape[1]
    slab_count = lax.axis_size("gx")
    band_count = lax.axis_size("gy")
    column = lax.axis_index("gx")
    band_index = lax.axis_index("gy")
    lon_total = slab_count * lon_dev
    lat_total = band_count * lat_dev
    taper_span = REACH * lon_dev + 1.0
    cell_ids = jnp.arange(cell_count, dtype=jnp.int32)
    cell_lon = column * lon_dev + cell_ids // (lat_dev * levels)
    cell_lat = band_index * lat_dev + cell_ids // levels % lat_dev
    obs_band = jnp.arange(obs_total, dtype=jnp.int32) // quarter

    def assimilate(batch_turn, carried):
        state_rows, mean_row = carried
        batch_id = order[batch_turn]
        root_slab = owner[batch_id]
        is_root = column == root_slab
        cells_of = obs_cell[batch_id]
        local_ids = lax.dynamic_slice_in_dim(cells_of, band_index * quarter, quarter)
        picked = jnp.take(state_rows, local_ids, axis=1)
        innovation = obs_value[batch_id] - jnp.take(mean_row, local_ids)
        root_rows = root_inv[batch_id]
        gain_rows = gain_inv[batch_id]
        joined = jnp.concatenate([picked, innovation[None, :]], axis=0)
        masked = jnp.where(is_root, joined, jnp.zeros_like(joined))
        joined = prior_direct(masked)
        picked, innovation = (joined[:members], joined[members])
        prior_all, innov_all = (
            lax.all_gather(picked, "gy", axis=1, tiled=True),
            lax.all_gather(innovation, "gy", axis=0, tiled=True),
        )
        weighted = product(prior_all, root_rows.T)
        gain_part = product(gain_rows, innov_all)
        weighted_all, gain_all = (
            lax.all_gather(weighted, "gy", axis=1, tiled=True),
            lax.all_gather(gain_part, "gy", axis=0, tiled=True),
        )
        obs_lon = root_slab * lon_dev + cells_of // (lat_dev * levels)
        obs_lat = obs_band * lat_dev + cells_of // levels % lat_dev
        slab_gap = jnp.abs(column - root_slab)
        in_reach = jnp.minimum(slab_gap, slab_count - slab_gap) <= REACH

        def near_update(operands):
            rows_now, mean_now = operands
            lon_gap = jnp.abs(obs_lon[:, None] - cell_lon[None, :])
            cycle_gap = jnp.minimum(lon_gap, lon_total - lon_gap)
            lat_gap = jnp.abs(obs_lat[:, None] - cell_lat[None, :])
            taper_rows = jnp.maximum(0.0, 1.0 - cycle_gap.astype(jnp.float32) / taper_span) * (
                1.0 - lat_gap.astype(jnp.float32) / lat_total
            )
            covariance = product(prior_all.T, rows_now) / (members - 1.0)
            gained = taper_rows * covariance
            stacked = jnp.concatenate([weighted_all, gain_all[None, :]], axis=0)
            increment = product(stacked, gained)
            return (rows_now - increment[:members], mean_now + increment[members])

        def keep_all(operands):
            return operands

        return lax.cond(in_reach, near_update, keep_all, (state_rows, mean_row))

    start_rows = anomalies.reshape(members, cell_count)
    start_mean = state_mean.reshape(cell_count)
    final_rows, final_mean = lax.fori_loop(0, BATCHES, assimilate, (start_rows, start_mean))
    return (
        final_rows.reshape(members, lon_dev, lat_dev, levels),
        final_mean.reshape(lon_dev, lat_dev, levels),
    )


def solution(mesh):
    return jax.shard_map(
        local,
        mesh=mesh,
        in_specs=(
            P(None, "gx", "gy", None),
            P("gx", "gy", None),
            P(None, "gy"),
            P(),
            P(),
            P(),
            P(None, "gy", None),
            P(None, "gy", None),
        ),
        out_specs=(P(None, "gx", "gy", None), P("gx", "gy", None)),
        check_vma=False,
    )
```

profile of v0, /device:TPU:0, one launch (start us, length us, event | category | flops | bytes accessed | tf_op | source)
XLA Modules:
  0.0 857.3 jit_solution(17424836850244703015)
XLA Ops:
  3.4 852.9 %while.19 = (s32[]{:T(128)}, f32[80,2048]{1,0:T(8,128)S(1)}, f32[2048]{0:T(1024)S(1)}, s32[16]{0:T(128)}, s32[16]{0:T(128)}, /*index=5*/s32[]{:T(128)}, s32[16,2...) while((s32[]{:T(128)}, f32[80,2048]{1,0:T(8,128)S(1)}, ...), condition=%wide.region_3.4_spmd.clone, body=%wide.region_0.3_spmd.clone.sunk | while | flops 1037555904 | bytes 10573724 | solution.py:98
  27.9 5.6 all-reduce.6
  34.7 6.7 all-reduce.7
  81.8 5.6 all-reduce.6
  88.7 6.1 all-reduce.7
  132.2 5.6 all-reduce.6
  139.1 6.6 all-reduce.7
  186.0 5.6 all-reduce.6
  192.9 6.1 all-reduce.7
  239.4 5.6 all-reduce.6
  246.2 6.6 all-reduce.7
  300.0 6.1 all-reduce.7
  353.4 6.6 all-reduce.7
  407.2 6.1 all-reduce.7
  453.7 5.6 all-reduce.6
  460.5 6.6 all-reduce.7
  507.5 5.6 all-reduce.6
  514.3 6.1 all-reduce.7
  567.7 6.6 all-reduce.7
  621.5 6.1 all-reduce.7
  674.8 6.6 all-reduce.7
  728.7 6.1 all-reduce.7
  779.1 6.6 all-reduce.7
  832.9 6.1 all-reduce.7
  (927 shorter events, 720.7 us)
Async XLA Ops:
  11.5 9.9 %collective-permute-start.5 = (f32[81,64]{0,1:T(8,128)S(1)}, f32[81,64]{0,1:T(8,128)S(1)}, u32[]{:S(2)}, u32[]{:S(2)}) collective-permute-start(f32[81,64]{0,1:T(8,128)S(1)} %maximum_select_fusion.2), channel_id=1, source_target_pairs={{0,4},{4,8},{8,12},{12,16},{16,20},{20,24},{24,28},{28,0},{1,5},{5... | collective-permute-start | bytes 62216 | tf_op jit(solution)/shard_map/while/body/eval_jaxpr/ppermute | solution.py:13
  14.5 12.8 %collective-permute-start.4 = (f32[81,64]{0,1:T(8,128)S(1)}, f32[81,64]{0,1:T(8,128)S(1)}, u32[]{:S(2)}, u32[]{:S(2)}) collective-permute-start(f32[81,64]{0,1:T(8,128)S(1)} %maximum_select_fusion.2), channel_id=1, source_target_pairs={{0,28},{4,0},{8,4},{12,8},{16,12},{20,16},{24,20},{28,24},{1,29},{... | collective-permute-start | bytes 62216 | tf_op jit(solution)/shard_map/while/body/eval_jaxpr/ppermute | solution.py:13
  17.6 9.7 %collective-permute-start.2 = (f32[81,64]{0,1:T(8,128)S(1)}, f32[81,64]{0,1:T(8,128)S(1)}, u32[]{:S(2)}, u32[]{:S(2)}) collective-permute-start(f32[81,64]{0,1:T(8,128)S(1)} %maximum_select_fusion.2), channel_id=1, source_target_pairs={{0,24},{4,28},{8,0},{12,4},{16,8},{20,12},{24,16},{28,20},{1,25},{... | collective-permute-start | bytes 62216 | tf_op jit(solution)/shard_map/while/body/eval_jaxpr/ppermute | solution.py:13
  67.2 14.1 %collective-permute-start.4 = (f32[81,64]{0,1:T(8,128)S(1)}, f32[81,64]{0,1:T(8,128)S(1)}, u32[]{:S(2)}, u32[]{:S(2)}) collective-permute-start(f32[81,64]{0,1:T(8,128)S(1)} %maximum_select_fusion.2), channel_id=1, source_target_pairs={{0,28},{4,0},{8,4},{12,8},{16,12},{20,16},{24,20},{28,24},{1,29},{... | collective-permute-start | bytes 62216 | tf_op jit(solution)/shard_map/while/body/eval_jaxpr/ppermute | solution.py:13
  114.8 11.7 %collective-permute-start.5 = (f32[81,64]{0,1:T(8,128)S(1)}, f32[81,64]{0,1:T(8,128)S(1)}, u32[]{:S(2)}, u32[]{:S(2)}) collective-permute-start(f32[81,64]{0,1:T(8,128)S(1)} %maximum_select_fusion.2), channel_id=1, source_target_pairs={{0,4},{4,8},{8,12},{12,16},{16,20},{20,24},{24,28},{28,0},{1,5},{5... | collective-permute-start | bytes 62216 | tf_op jit(solution)/shard_map/while/body/eval_jaxpr/ppermute | solution.py:13
  119.2 12.0 %collective-permute-start.4 = (f32[81,64]{0,1:T(8,128)S(1)}, f32[81,64]{0,1:T(8,128)S(1)}, u32[]{:S(2)}, u32[]{:S(2)}) collective-permute-start(f32[81,64]{0,1:T(8,128)S(1)} %maximum_select_fusion.2), channel_id=1, source_target_pairs={{0,28},{4,0},{8,4},{12,8},{16,12},{20,16},{24,20},{28,24},{1,29},{... | collective-permute-start | bytes 62216 | tf_op jit(solution)/shard_map/while/body/eval_jaxpr/ppermute | solution.py:13
  173.1 12.4 %collective-permute-start.4 = (f32[81,64]{0,1:T(8,128)S(1)}, f32[81,64]{0,1:T(8,128)S(1)}, u32[]{:S(2)}, u32[]{:S(2)}) collective-permute-start(f32[81,64]{0,1:T(8,128)S(1)} %maximum_select_fusion.2), channel_id=1, source_target_pairs={{0,28},{4,0},{8,4},{12,8},{16,12},{20,16},{24,20},{28,24},{1,29},{... | collective-permute-start | bytes 62216 | tf_op jit(solution)/shard_map/while/body/eval_jaxpr/ppermute | solution.py:13
  175.8 9.7 %collective-permute-start.2 = (f32[81,64]{0,1:T(8,128)S(1)}, f32[81,64]{0,1:T(8,128)S(1)}, u32[]{:S(2)}, u32[]{:S(2)}) collective-permute-start(f32[81,64]{0,1:T(8,128)S(1)} %maximum_select_fusion.2), channel_id=1, source_target_pairs={{0,24},{4,28},{8,0},{12,4},{16,8},{20,12},{24,16},{28,20},{1,25},{... | collective-permute-start | bytes 62216 | tf_op jit(solution)/shard_map/while/body/eval_jaxpr/ppermute | solution.py:13
  224.6 14.2 %collective-permute-start.4 = (f32[81,64]{0,1:T(8,128)S(1)}, f32[81,64]{0,1:T(8,128)S(1)}, u32[]{:S(2)}, u32[]{:S(2)}) collective-permute-start(f32[81,64]{0,1:T(8,128)S(1)} %maximum_select_fusion.2), channel_id=1, source_target_pairs={{0,28},{4,0},{8,4},{12,8},{16,12},{20,16},{24,20},{28,24},{1,29},{... | collective-permute-start | bytes 62216 | tf_op jit(solution)/shard_map/while/body/eval_jaxpr/ppermute | solution.py:13
  278.2 14.4 %collective-permute-start.4 = (f32[81,64]{0,1:T(8,128)S(1)}, f32[81,64]{0,1:T(8,128)S(1)}, u32[]{:S(2)}, u32[]{:S(2)}) collective-permute-start(f32[81,64]{0,1:T(8,128)S(1)} %maximum_select_fusion.2), channel_id=1, source_target_pairs={{0,28},{4,0},{8,4},{12,8},{16,12},{20,16},{24,20},{28,24},{1,29},{... | collective-permute-start | bytes 62216 | tf_op jit(solution)/shard_map/while/body/eval_jaxpr/ppermute | solution.py:13
  331.6 14.4 %collective-permute-start.4 = (f32[81,64]{0,1:T(8,128)S(1)}, f32[81,64]{0,1:T(8,128)S(1)}, u32[]{:S(2)}, u32[]{:S(2)}) collective-permute-start(f32[81,64]{0,1:T(8,128)S(1)} %maximum_select_fusion.2), channel_id=1, source_target_pairs={{0,28},{4,0},{8,4},{12,8},{16,12},{20,16},{24,20},{28,24},{1,29},{... | collective-permute-start | bytes 62216 | tf_op jit(solution)/shard_map/while/body/eval_jaxpr/ppermute | solution.py:13
  336.3 9.7 %collective-permute-start.2 = (f32[81,64]{0,1:T(8,128)S(1)}, f32[81,64]{0,1:T(8,128)S(1)}, u32[]{:S(2)}, u32[]{:S(2)}) collective-permute-start(f32[81,64]{0,1:T(8,128)S(1)} %maximum_select_fusion.2), channel_id=1, source_target_pairs={{0,24},{4,28},{8,0},{12,4},{16,8},{20,12},{24,16},{28,20},{1,25},{... | collective-permute-start | bytes 62216 | tf_op jit(solution)/shard_map/while/body/eval_jaxpr/ppermute | solution.py:13
  385.4 14.4 %collective-permute-start.4 = (f32[81,64]{0,1:T(8,128)S(1)}, f32[81,64]{0,1:T(8,128)S(1)}, u32[]{:S(2)}, u32[]{:S(2)}) collective-permute-start(f32[81,64]{0,1:T(8,128)S(1)} %maximum_select_fusion.2), channel_id=1, source_target_pairs={{0,28},{4,0},{8,4},{12,8},{16,12},{20,16},{24,20},{28,24},{1,29},{... | collective-permute-start | bytes 62216 | tf_op jit(solution)/shard_map/while/body/eval_jaxpr/ppermute | solution.py:13
  438.7 14.4 %collective-permute-start.4 = (f32[81,64]{0,1:T(8,128)S(1)}, f32[81,64]{0,1:T(8,128)S(1)}, u32[]{:S(2)}, u32[]{:S(2)}) collective-permute-start(f32[81,64]{0,1:T(8,128)S(1)} %maximum_select_fusion.2), channel_id=1, source_target_pairs={{0,28},{4,0},{8,4},{12,8},{16,12},{20,16},{24,20},{28,24},{1,29},{... | collective-permute-start | bytes 62216 | tf_op jit(solution)/shard_map/while/body/eval_jaxpr/ppermute | solution.py:13
  443.4 9.7 %collective-permute-start.2 = (f32[81,64]{0,1:T(8,128)S(1)}, f32[81,64]{0,1:T(8,128)S(1)}, u32[]{:S(2)}, u32[]{:S(2)}) collective-permute-start(f32[81,64]{0,1:T(8,128)S(1)} %maximum_select_fusion.2), channel_id=1, source_target_pairs={{0,24},{4,28},{8,0},{12,4},{16,8},{20,12},{24,16},{28,20},{1,25},{... | collective-permute-start | bytes 62216 | tf_op jit(solution)/shard_map/while/body/eval_jaxpr/ppermute | solution.py:13
  492.5 14.4 %collective-permute-start.4 = (f32[81,64]{0,1:T(8,128)S(1)}, f32[81,64]{0,1:T(8,128)S(1)}, u32[]{:S(2)}, u32[]{:S(2)}) collective-permute-start(f32[81,64]{0,1:T(8,128)S(1)} %maximum_select_fusion.2), channel_id=1, source_target_pairs={{0,28},{4,0},{8,4},{12,8},{16,12},{20,16},{24,20},{28,24},{1,29},{... | collective-permute-start | bytes 62216 | tf_op jit(solution)/shard_map/while/body/eval_jaxpr/ppermute | solution.py:13
  497.2 9.7 %collective-permute-start.2 = (f32[81,64]{0,1:T(8,128)S(1)}, f32[81,64]{0,1:T(8,128)S(1)}, u32[]{:S(2)}, u32[]{:S(2)}) collective-permute-start(f32[81,64]{0,1:T(8,128)S(1)} %maximum_select_fusion.2), channel_id=1, source_target_pairs={{0,24},{4,28},{8,0},{12,4},{16,8},{20,12},{24,16},{28,20},{1,25},{... | collective-permute-start | bytes 62216 | tf_op jit(solution)/shard_map/while/body/eval_jaxpr/ppermute | solution.py:13
  545.9 14.4 %collective-permute-start.4 = (f32[81,64]{0,1:T(8,128)S(1)}, f32[81,64]{0,1:T(8,128)S(1)}, u32[]{:S(2)}, u32[]{:S(2)}) collective-permute-start(f32[81,64]{0,1:T(8,128)S(1)} %maximum_select_fusion.2), channel_id=1, source_target_pairs={{0,28},{4,0},{8,4},{12,8},{16,12},{20,16},{24,20},{28,24},{1,29},{... | collective-permute-start | bytes 62216 | tf_op jit(solution)/shard_map/while/body/eval_jaxpr/ppermute | solution.py:13
  599.7 14.4 %collective-permute-start.4 = (f32[81,64]{0,1:T(8,128)S(1)}, f32[81,64]{0,1:T(8,128)S(1)}, u32[]{:S(2)}, u32[]{:S(2)}) collective-permute-start(f32[81,64]{0,1:T(8,128)S(1)} %maximum_select_fusion.2), channel_id=1, source_target_pairs={{0,28},{4,0},{8,4},{12,8},{16,12},{20,16},{24,20},{28,24},{1,29},{... | collective-permute-start | bytes 62216 | tf_op jit(solution)/shard_map/while/body/eval_jaxpr/ppermute | solution.py:13
  653.0 14.4 %collective-permute-start.4 = (f32[81,64]{0,1:T(8,128)S(1)}, f32[81,64]{0,1:T(8,128)S(1)}, u32[]{:S(2)}, u32[]{:S(2)}) collective-permute-start(f32[81,64]{0,1:T(8,128)S(1)} %maximum_select_fusion.2), channel_id=1, source_target_pairs={{0,28},{4,0},{8,4},{12,8},{16,12},{20,16},{24,20},{28,24},{1,29},{... | collective-permute-start | bytes 62216 | tf_op jit(solution)/shard_map/while/body/eval_jaxpr/ppermute | solution.py:13
  706.8 14.4 %collective-permute-start.4 = (f32[81,64]{0,1:T(8,128)S(1)}, f32[81,64]{0,1:T(8,128)S(1)}, u32[]{:S(2)}, u32[]{:S(2)}) collective-permute-start(f32[81,64]{0,1:T(8,128)S(1)} %maximum_select_fusion.2), channel_id=1, source_target_pairs={{0,28},{4,0},{8,4},{12,8},{16,12},{20,16},{24,20},{28,24},{1,29},{... | collective-permute-start | bytes 62216 | tf_op jit(solution)/shard_map/while/body/eval_jaxpr/ppermute | solution.py:13
  754.8 11.7 %collective-permute-start.5 = (f32[81,64]{0,1:T(8,128)S(1)}, f32[81,64]{0,1:T(8,128)S(1)}, u32[]{:S(2)}, u32[]{:S(2)}) collective-permute-start(f32[81,64]{0,1:T(8,128)S(1)} %maximum_select_fusion.2), channel_id=1, source_target_pairs={{0,4},{4,8},{8,12},{12,16},{16,20},{20,24},{24,28},{28,0},{1,5},{5... | collective-permute-start | bytes 62216 | tf_op jit(solution)/shard_map/while/body/eval_jaxpr/ppermute | solution.py:13
  759.3 12.0 %collective-permute-start.4 = (f32[81,64]{0,1:T(8,128)S(1)}, f32[81,64]{0,1:T(8,128)S(1)}, u32[]{:S(2)}, u32[]{:S(2)}) collective-permute-start(f32[81,64]{0,1:T(8,128)S(1)} %maximum_select_fusion.2), channel_id=1, source_target_pairs={{0,28},{4,0},{8,4},{12,8},{16,12},{20,16},{24,20},{28,24},{1,29},{... | collective-permute-start | bytes 62216 | tf_op jit(solution)/shard_map/while/body/eval_jaxpr/ppermute | solution.py:13
  813.1 12.4 %collective-permute-start.4 = (f32[81,64]{0,1:T(8,128)S(1)}, f32[81,64]{0,1:T(8,128)S(1)}, u32[]{:S(2)}, u32[]{:S(2)}) collective-permute-start(f32[81,64]{0,1:T(8,128)S(1)} %maximum_select_fusion.2), channel_id=1, source_target_pairs={{0,28},{4,0},{8,4},{12,8},{16,12},{20,16},{24,20},{28,24},{1,29},{... | collective-permute-start | bytes 62216 | tf_op jit(solution)/shard_map/while/body/eval_jaxpr/ppermute | solution.py:13
  (89 other events, 901.5 us)
where the time goes:
time: 862 us; the launch traced here: 857 us
  blocking collectives  365 us (42%)
  starting transfers between devices  204 us (24%)
  local copies, waits for them, and re-layouts  113 us (13%)
  matrix products  94.3 us (11%)
  loops' own time  70.2 us (8%)
  other arithmetic  8.9 us (1%)
    ppermute x96, starting transfers between devices, shifted(): return lax.ppermute(value, axis, pairs)  204 us
    while x16, blocking collectives  102 us
    dot_general x60, matrix products, product(): jnp.dot(left_side, right_side, precision=lax.Precision.HIGHEST, preferred...  94.3 us
    all_gather x16, blocking collectives, assimilate(): lax.all_gather(innovation, 'gy', axis=0, tiled=True)  90.1 us
    all_gather x16, blocking collectives, assimilate(): lax.all_gather(weighted, 'gy', axis=1, tiled=True)  86.7 us
    all_gather x16, blocking collectives, assimilate(): lax.all_gather(picked, 'gy', axis=1, tiled=True)  86.4 us
    another operation x1, loops' own time, local(): lax.fori_loop(0, BATCHES, assimilate, (start_rows, start_mean))  60.8 us
    while x128, local copies, waits for them, and re-layouts  22.2 us
  transfers between devices with their start and end apart: 96, of which 4 were waited for; matrix products, arithmetic and copies ran while one was open for 1% of the time, Pallas kernels for 0%

commit v1 on v0

--- a/solution.py
+++ b/solution.py
@@ -5,6 +5,18 @@
 
 BATCHES = 16
 REACH = 3
+
+
+def gather_by_bits(x, axis, dim):
+    ways, here = (lax.axis_size(axis), lax.axis_index(axis))
+    grown, reach = (x, 1)
+    while reach < ways:
+        theirs = lax.ppermute(grown, axis, [(d, d ^ reach) for d in range(ways)])
+        mine_first = jnp.concatenate([grown, theirs], axis=dim)
+        theirs_first = jnp.concatenate([theirs, grown], axis=dim)
+        grown = jnp.where(here & reach == 0, mine_first, theirs_first)
+        reach = 2 * reach
+    return grown
 
 
 def shifted(value, axis, steps):
@@ -66,7 +78,7 @@
         weighted = product(prior_all, root_rows.T)
         gain_part = product(gain_rows, innov_all)
         weighted_all, gain_all = (
-            lax.all_gather(weighted, "gy", axis=1, tiled=True),
+            gather_by_bits(weighted, "gy", 1),
             lax.all_gather(gain_part, "gy", axis=0, tiled=True),
         )
         obs_lon = root_slab * lon_dev + cells_of // (lat_dev * levels)

time: 862 us -> 815 us (0.945)
  blocking collectives: 365 us -> 291 us
  starting transfers between devices: 204 us -> 218 us
  loops' own time: 70.2 us -> 79.9 us
    all_gather x16 -> x0, blocking collectives: 86.7 us -> none  [assimilate(): lax.all_gather(weighted, 'gy', axis=1, tiled=True)]
    all_gather x16, blocking collectives: 90.1 us -> 114 us  [assimilate(): lax.all_gather(innovation, 'gy', axis=0, tiled=True)]
    ppermute x0 -> x32, starting transfers between devices: none -> 14 us  [gather_by_bits(): theirs = lax.ppermute(grown, axis, [(d, d ^ reach) for d in range(ways)])]
    while x16, blocking collectives: 102 us -> 90.1 us
  transfers between devices with their start and end apart: 96 -> 128, of which waited for: 4 -> 2; matrix products, arithmetic and copies ran while one was open for 1% -> 5% of each run, Pallas kernels for 0% -> 0%
where the time goes in v1:
time: 815 us; the launch traced here: 811 us
  blocking collectives  291 us (36%)
  starting transfers between devices  218 us (27%)
  local copies, waits for them, and re-layouts  117 us (14%)
  matrix products  94.3 us (12%)
  loops' own time  79.9 us (10%)
  other arithmetic  9.55 us (1%)
    ppermute x96, starting transfers between devices, shifted(): return lax.ppermute(value, axis, pairs)  204 us
    all_gather x16, blocking collectives, assimilate(): lax.all_gather(innovation, 'gy', axis=0, tiled=True)  114 us
    dot_general x60, matrix products, product(): jnp.dot(left_side, right_side, precision=lax.Precision.HIGHEST, preferred...  94.3 us
    while x16, blocking collectives  90.1 us
    all_gather x16, blocking collectives, assimilate(): lax.all_gather(picked, 'gy', axis=1, tiled=True)  86.7 us
    another operation x1, loops' own time, local(): lax.fori_loop(0, BATCHES, assimilate, (start_rows, start_mean))  69.1 us
    while x128, local copies, waits for them, and re-layouts  23.1 us
    dynamic_slice x16, local copies, waits for them, and re-layouts, assimilate(): root_slab = owner[batch_id]  21.2 us
  transfers between devices with their start and end apart: 128, of which 2 were waited for; matrix products, arithmetic and copies ran while one was open for 5% of the time, Pallas kernels for 0%

profile of v1, /device:TPU:0, one launch (start us, length us, event | category | flops | bytes accessed | tf_op | source)
XLA Modules:
  0.0 810.5 jit_solution(12496090137538716553)
XLA Ops:
  3.4 806.1 %while.19 = (s32[]{:T(128)}, f32[80,2048]{1,0:T(8,128)S(1)}, f32[2048]{0:T(1024)S(1)}, s32[16]{0:T(128)}, s32[16]{0:T(128)}, /*index=5*/s32[]{:T(128)}, s32[16,2...) while((s32[]{:T(128)}, f32[80,2048]{1,0:T(8,128)S(1)}, ...), condition=%wide.region_3.4_spmd.clone, body=%wide.region_0.3_spmd.clone.sunk | while | flops 1037648064 | bytes 11454532 | solution.py:110
  35.4 7.0 all-reduce.6
  44.1 5.6 all-reduce.7
  86.0 7.1 all-reduce.6
  94.8 5.6 all-reduce.7
  133.4 7.1 all-reduce.6
  184.1 7.1 all-reduce.6
  192.9 5.6 all-reduce.7
  234.8 7.1 all-reduce.6
  285.6 7.1 all-reduce.6
  336.3 7.1 all-reduce.6
  387.0 7.1 all-reduce.6
  395.8 5.6 all-reduce.7
  437.7 7.1 all-reduce.6
  488.5 7.1 all-reduce.6
  497.3 5.6 all-reduce.7
  539.2 7.1 all-reduce.6
  589.9 7.1 all-reduce.6
  640.6 7.1 all-reduce.6
  691.4 7.1 all-reduce.6
  738.7 7.1 all-reduce.6
  747.5 5.6 all-reduce.7
  789.4 7.1 all-reduce.6
  798.3 5.6 all-reduce.7
  (1035 shorter events, 654.9 us)
Async XLA Ops:
  12.0 9.9 %collective-permute-start.5 = (f32[81,64]{0,1:T(8,128)S(1)}, f32[81,64]{0,1:T(8,128)S(1)}, u32[]{:S(2)}, u32[]{:S(2)}) collective-permute-start(f32[81,64]{0,1:T(8,128)S(1)} %maximum_select_fusion.4), channel_id=1, source_target_pairs={{0,4},{4,8},{8,12},{12,16},{16,20},{20,24},{24,28},{28,0},{1,5},{5... | collective-permute-start | bytes 62216 | tf_op jit(solution)/shard_map/while/body/eval_jaxpr/ppermute | solution.py:25
  15.0 13.0 %collective-permute-start.4 = (f32[81,64]{0,1:T(8,128)S(1)}, f32[81,64]{0,1:T(8,128)S(1)}, u32[]{:S(2)}, u32[]{:S(2)}) collective-permute-start(f32[81,64]{0,1:T(8,128)S(1)} %maximum_select_fusion.4), channel_id=1, source_target_pairs={{0,28},{4,0},{8,4},{12,8},{16,12},{20,16},{24,20},{28,24},{1,29},{... | collective-permute-start | bytes 62216 | tf_op jit(solution)/shard_map/while/body/eval_jaxpr/ppermute | solution.py:25
  18.1 9.9 %collective-permute-start.2 = (f32[81,64]{0,1:T(8,128)S(1)}, f32[81,64]{0,1:T(8,128)S(1)}, u32[]{:S(2)}, u32[]{:S(2)}) collective-permute-start(f32[81,64]{0,1:T(8,128)S(1)} %maximum_select_fusion.4), channel_id=1, source_target_pairs={{0,24},{4,28},{8,0},{12,4},{16,8},{20,12},{24,16},{28,20},{1,25},{... | collective-permute-start | bytes 62216 | tf_op jit(solution)/shard_map/while/body/eval_jaxpr/ppermute | solution.py:25
  64.2 14.4 %collective-permute-start.4 = (f32[81,64]{0,1:T(8,128)S(1)}, f32[81,64]{0,1:T(8,128)S(1)}, u32[]{:S(2)}, u32[]{:S(2)}) collective-permute-start(f32[81,64]{0,1:T(8,128)S(1)} %maximum_select_fusion.4), channel_id=1, source_target_pairs={{0,28},{4,0},{8,4},{12,8},{16,12},{20,16},{24,20},{28,24},{1,29},{... | collective-permute-start | bytes 62216 | tf_op jit(solution)/shard_map/while/body/eval_jaxpr/ppermute | solution.py:25
  68.7 9.9 %collective-permute-start.2 = (f32[81,64]{0,1:T(8,128)S(1)}, f32[81,64]{0,1:T(8,128)S(1)}, u32[]{:S(2)}, u32[]{:S(2)}) collective-permute-start(f32[81,64]{0,1:T(8,128)S(1)} %maximum_select_fusion.4), channel_id=1, source_target_pairs={{0,24},{4,28},{8,0},{12,4},{16,8},{20,12},{24,16},{28,20},{1,25},{... | collective-permute-start | bytes 62216 | tf_op jit(solution)/shard_map/while/body/eval_jaxpr/ppermute | solution.py:25
  109.1 11.7 %collective-permute-start.5 = (f32[81,64]{0,1:T(8,128)S(1)}, f32[81,64]{0,1:T(8,128)S(1)}, u32[]{:S(2)}, u32[]{:S(2)}) collective-permute-start(f32[81,64]{0,1:T(8,128)S(1)} %maximum_select_fusion.4), channel_id=1, source_target_pairs={{0,4},{4,8},{8,12},{12,16},{16,20},{20,24},{24,28},{28,0},{1,5},{5... | collective-permute-start | bytes 62216 | tf_op jit(solution)/shard_map/while/body/eval_jaxpr/ppermute | solution.py:25
  113.7 12.1 %collective-permute-start.4 = (f32[81,64]{0,1:T(8,128)S(1)}, f32[81,64]{0,1:T(8,128)S(1)}, u32[]{:S(2)}, u32[]{:S(2)}) collective-permute-start(f32[81,64]{0,1:T(8,128)S(1)} %maximum_select_fusion.4), channel_id=1, source_target_pairs={{0,28},{4,0},{8,4},{12,8},{16,12},{20,16},{24,20},{28,24},{1,29},{... | collective-permute-start | bytes 62216 | tf_op jit(solution)/shard_map/while/body/eval_jaxpr/ppermute | solution.py:25
  164.1 12.6 %collective-permute-start.4 = (f32[81,64]{0,1:T(8,128)S(1)}, f32[81,64]{0,1:T(8,128)S(1)}, u32[]{:S(2)}, u32[]{:S(2)}) collective-permute-start(f32[81,64]{0,1:T(8,128)S(1)} %maximum_select_fusion.4), channel_id=1, source_target_pairs={{0,28},{4,0},{8,4},{12,8},{16,12},{20,16},{24,20},{28,24},{1,29},{... | collective-permute-start | bytes 62216 | tf_op jit(solution)/shard_map/while/body/eval_jaxpr/ppermute | solution.py:25
  166.8 9.9 %collective-permute-start.2 = (f32[81,64]{0,1:T(8,128)S(1)}, f32[81,64]{0,1:T(8,128)S(1)}, u32[]{:S(2)}, u32[]{:S(2)}) collective-permute-start(f32[81,64]{0,1:T(8,128)S(1)} %maximum_select_fusion.4), channel_id=1, source_target_pairs={{0,24},{4,28},{8,0},{12,4},{16,8},{20,12},{24,16},{28,20},{1,25},{... | collective-permute-start | bytes 62216 | tf_op jit(solution)/shard_map/while/body/eval_jaxpr/ppermute | solution.py:25
  213.0 14.4 %collective-permute-start.4 = (f32[81,64]{0,1:T(8,128)S(1)}, f32[81,64]{0,1:T(8,128)S(1)}, u32[]{:S(2)}, u32[]{:S(2)}) collective-permute-start(f32[81,64]{0,1:T(8,128)S(1)} %maximum_select_fusion.4), channel_id=1, source_target_pairs={{0,28},{4,0},{8,4},{12,8},{16,12},{20,16},{24,20},{28,24},{1,29},{... | collective-permute-start | bytes 62216 | tf_op jit(solution)/shard_map/while/body/eval_jaxpr/ppermute | solution.py:25
  217.5 9.9 %collective-permute-start.2 = (f32[81,64]{0,1:T(8,128)S(1)}, f32[81,64]{0,1:T(8,128)S(1)}, u32[]{:S(2)}, u32[]{:S(2)}) collective-permute-start(f32[81,64]{0,1:T(8,128)S(1)} %maximum_select_fusion.4), channel_id=1, source_target_pairs={{0,24},{4,28},{8,0},{12,4},{16,8},{20,12},{24,16},{28,20},{1,25},{... | collective-permute-start | bytes 62216 | tf_op jit(solution)/shard_map/while/body/eval_jaxpr/ppermute | solution.py:25
  263.5 14.6 %collective-permute-start.4 = (f32[81,64]{0,1:T(8,128)S(1)}, f32[81,64]{0,1:T(8,128)S(1)}, u32[]{:S(2)}, u32[]{:S(2)}) collective-permute-start(f32[81,64]{0,1:T(8,128)S(1)} %maximum_select_fusion.4), channel_id=1, source_target_pairs={{0,28},{4,0},{8,4},{12,8},{16,12},{20,16},{24,20},{28,24},{1,29},{... | collective-permute-start | bytes 62216 | tf_op jit(solution)/shard_map/while/body/eval_jaxpr/ppermute | solution.py:25
  314.2 14.6 %collective-permute-start.4 = (f32[81,64]{0,1:T(8,128)S(1)}, f32[81,64]{0,1:T(8,128)S(1)}, u32[]{:S(2)}, u32[]{:S(2)}) collective-permute-start(f32[81,64]{0,1:T(8,128)S(1)} %maximum_select_fusion.4), channel_id=1, source_target_pairs={{0,28},{4,0},{8,4},{12,8},{16,12},{20,16},{24,20},{28,24},{1,29},{... | collective-permute-start | bytes 62216 | tf_op jit(solution)/shard_map/while/body/eval_jaxpr/ppermute | solution.py:25
  364.9 14.6 %collective-permute-start.4 = (f32[81,64]{0,1:T(8,128)S(1)}, f32[81,64]{0,1:T(8,128)S(1)}, u32[]{:S(2)}, u32[]{:S(2)}) collective-permute-start(f32[81,64]{0,1:T(8,128)S(1)} %maximum_select_fusion.4), channel_id=1, source_target_pairs={{0,28},{4,0},{8,4},{12,8},{16,12},{20,16},{24,20},{28,24},{1,29},{... | collective-permute-start | bytes 62216 | tf_op jit(solution)/shard_map/while/body/eval_jaxpr/ppermute | solution.py:25
  415.7 14.6 %collective-permute-start.4 = (f32[81,64]{0,1:T(8,128)S(1)}, f32[81,64]{0,1:T(8,128)S(1)}, u32[]{:S(2)}, u32[]{:S(2)}) collective-permute-start(f32[81,64]{0,1:T(8,128)S(1)} %maximum_select_fusion.4), channel_id=1, source_target_pairs={{0,28},{4,0},{8,4},{12,8},{16,12},{20,16},{24,20},{28,24},{1,29},{... | collective-permute-start | bytes 62216 | tf_op jit(solution)/shard_map/while/body/eval_jaxpr/ppermute | solution.py:25
  420.4 9.9 %collective-permute-start.2 = (f32[81,64]{0,1:T(8,128)S(1)}, f32[81,64]{0,1:T(8,128)S(1)}, u32[]{:S(2)}, u32[]{:S(2)}) collective-permute-start(f32[81,64]{0,1:T(8,128)S(1)} %maximum_select_fusion.4), channel_id=1, source_target_pairs={{0,24},{4,28},{8,0},{12,4},{16,8},{20,12},{24,16},{28,20},{1,25},{... | collective-permute-start | bytes 62216 | tf_op jit(solution)/shard_map/while/body/eval_jaxpr/ppermute | solution.py:25
  466.4 14.6 %collective-permute-start.4 = (f32[81,64]{0,1:T(8,128)S(1)}, f32[81,64]{0,1:T(8,128)S(1)}, u32[]{:S(2)}, u32[]{:S(2)}) collective-permute-start(f32[81,64]{0,1:T(8,128)S(1)} %maximum_select_fusion.4), channel_id=1, source_target_pairs={{0,28},{4,0},{8,4},{12,8},{16,12},{20,16},{24,20},{28,24},{1,29},{... | collective-permute-start | bytes 62216 | tf_op jit(solution)/shard_map/while/body/eval_jaxpr/ppermute | solution.py:25
  517.1 14.6 %collective-permute-start.4 = (f32[81,64]{0,1:T(8,128)S(1)}, f32[81,64]{0,1:T(8,128)S(1)}, u32[]{:S(2)}, u32[]{:S(2)}) collective-permute-start(f32[81,64]{0,1:T(8,128)S(1)} %maximum_select_fusion.4), channel_id=1, source_target_pairs={{0,28},{4,0},{8,4},{12,8},{16,12},{20,16},{24,20},{28,24},{1,29},{... | collective-permute-start | bytes 62216 | tf_op jit(solution)/shard_map/while/body/eval_jaxpr/ppermute | solution.py:25
  567.8 14.6 %collective-permute-start.4 = (f32[81,64]{0,1:T(8,128)S(1)}, f32[81,64]{0,1:T(8,128)S(1)}, u32[]{:S(2)}, u32[]{:S(2)}) collective-permute-start(f32[81,64]{0,1:T(8,128)S(1)} %maximum_select_fusion.4), channel_id=1, source_target_pairs={{0,28},{4,0},{8,4},{12,8},{16,12},{20,16},{24,20},{28,24},{1,29},{... | collective-permute-start | bytes 62216 | tf_op jit(solution)/shard_map/while/body/eval_jaxpr/ppermute | solution.py:25
  618.6 14.6 %collective-permute-start.4 = (f32[81,64]{0,1:T(8,128)S(1)}, f32[81,64]{0,1:T(8,128)S(1)}, u32[]{:S(2)}, u32[]{:S(2)}) collective-permute-start(f32[81,64]{0,1:T(8,128)S(1)} %maximum_select_fusion.4), channel_id=1, source_target_pairs={{0,28},{4,0},{8,4},{12,8},{16,12},{20,16},{24,20},{28,24},{1,29},{... | collective-permute-start | bytes 62216 | tf_op jit(solution)/shard_map/while/body/eval_jaxpr/ppermute | solution.py:25
  669.3 14.6 %collective-permute-start.4 = (f32[81,64]{0,1:T(8,128)S(1)}, f32[81,64]{0,1:T(8,128)S(1)}, u32[]{:S(2)}, u32[]{:S(2)}) collective-permute-start(f32[81,64]{0,1:T(8,128)S(1)} %maximum_select_fusion.4), channel_id=1, source_target_pairs={{0,28},{4,0},{8,4},{12,8},{16,12},{20,16},{24,20},{28,24},{1,29},{... | collective-permute-start | bytes 62216 | tf_op jit(solution)/shard_map/while/body/eval_jaxpr/ppermute | solution.py:25
  714.4 11.7 %collective-permute-start.5 = (f32[81,64]{0,1:T(8,128)S(1)}, f32[81,64]{0,1:T(8,128)S(1)}, u32[]{:S(2)}, u32[]{:S(2)}) collective-permute-start(f32[81,64]{0,1:T(8,128)S(1)} %maximum_select_fusion.4), channel_id=1, source_target_pairs={{0,4},{4,8},{8,12},{12,16},{16,20},{20,24},{24,28},{28,0},{1,5},{5... | collective-permute-start | bytes 62216 | tf_op jit(solution)/shard_map/while/body/eval_jaxpr/ppermute | solution.py:25
  719.0 12.1 %collective-permute-start.4 = (f32[81,64]{0,1:T(8,128)S(1)}, f32[81,64]{0,1:T(8,128)S(1)}, u32[]{:S(2)}, u32[]{:S(2)}) collective-permute-start(f32[81,64]{0,1:T(8,128)S(1)} %maximum_select_fusion.4), channel_id=1, source_target_pairs={{0,28},{4,0},{8,4},{12,8},{16,12},{20,16},{24,20},{28,24},{1,29},{... | collective-permute-start | bytes 62216 | tf_op jit(solution)/shard_map/while/body/eval_jaxpr/ppermute | solution.py:25
  769.4 12.6 %collective-permute-start.4 = (f32[81,64]{0,1:T(8,128)S(1)}, f32[81,64]{0,1:T(8,128)S(1)}, u32[]{:S(2)}, u32[]{:S(2)}) collective-permute-start(f32[81,64]{0,1:T(8,128)S(1)} %maximum_select_fusion.4), channel_id=1, source_target_pairs={{0,28},{4,0},{8,4},{12,8},{16,12},{20,16},{24,20},{28,24},{1,29},{... | collective-permute-start | bytes 62216 | tf_op jit(solution)/shard_map/while/body/eval_jaxpr/ppermute | solution.py:25
  (121 other events, 1165.3 us)
